TPU v7x, 32 devices: a whole 2x2x4 slice. The times are simulated.
32 devices in a mesh: grp: 8 (over z, y), col: 4 (over x, core).
Axes of the slice: x: 2, y: 2, z: 4, core: 2. Of those that a mesh axis runs over, the one named last changes fastest.
Arguments:
- features: bfloat16 [65536, 256], P(('grp', 'col')), may hold values from -6 to 6
- adj_tiles: bfloat16 [1536, 256, 256], P('grp'), may hold values from 0 to 1.5
- block_pairs: int32 [8, 192, 2], P('grp'), may hold values from 0 to 31, as said below
- tile_count: int32 [8], P('grp'), may hold values from 32 to 192, as said below
- degree: int32 [65536], P('grp'), may hold values from 1 to 769
- labels: int32 [65536], P(('grp', 'col')), may hold values from 0 to 63
- loss_mask: int32 [65536], P(('grp', 'col')), may hold values from 0 to 1
- slot_piece: int32 [8, 79], replicated, may hold values from -1 to 416, as said below
- master: float32 [632, 2, 256], P('grp', None, 'col'), may hold values from -4 to 4
- moment_one: float32 [632, 2, 256], P('grp', None, 'col'), may hold values from -0.125 to 0.125
- moment_two: float32 [632, 2, 256], P('grp', None, 'col'), may hold values from 3.0517579e-06 to 0.00030517578
Outputs:
- mean_loss: float32 [], replicated
- new_master: float32 [632, 2, 256], P('grp', None, 'col')
- new_moment_one: float32 [632, 2, 256], P('grp', None, 'col')
- new_moment_two: float32 [632, 2, 256], P('grp', None, 'col')
- new_weights: bfloat16 [632, 2, 256], P('grp', None, 'col')
Inputs may be any that keep to these rules, and one draw needn't show every extreme that they name: `block_pairs`: of each group, the first tile_count entries are distinct pairs of blocks and include every diagonal pair (r, r); later entries are padding. `tile_count`: some group has 192 live tiles in every draw. `slot_piece`: each piece 0 to 416 sits in exactly one slot; a group holds at most 79 pieces, and some group holds 79 in every draw.
All inputs are finite; a program needn't handle non-finite values.
Results may differ from a plain program's by a relative error of at most 0.0079.
Values may be sent and summed in bfloat16 or wider, within the bound.
A program may use at most 128 MiB of HBM per device.

v0:
```python
import jax
import jax.numpy as jnp
from jax import lax
from jax.sharding import PartitionSpec as P

F = 256
HID = 256
CLS = 64
B = 256
PR = 2
STEP = 7
PROWS = 834
PIECES = 417
learn_rate = 0.01
beta_one = 0.5
beta_two = 0.5
adam_epsilon = 1e-08
decay_rate = 0.1


def contract_rows(left, right):
    return lax.dot_general(
        left, right, (((0,), (0,)), ((), ())), preferred_element_type=jnp.float32
    )


def contract_cols(left, right):
    return lax.dot_general(
        left, right, (((1,), (1,)), ((), ())), preferred_element_type=jnp.float32
    )


def body(
    features,
    adj_tiles,
    block_pairs,
    tile_count,
    degree,
    labels,
    loss_mask,
    slot_piece,
    master,
    moment_one,
    moment_two,
):
    col_count = lax.axis_size("col")
    grp_count = lax.axis_size("grp")
    col_index = lax.axis_index("col")
    grp_index = lax.axis_index("grp")
    node_rows = features.shape[0]
    group_nodes = degree.shape[0]
    block_count = group_nodes // B
    tile_slots = adj_tiles.shape[0]
    slot_width = slot_piece.shape[1]
    col_width = master.shape[2]
    own_slots = master.astype(jnp.bfloat16)[None]
    gathered = lax.all_gather(own_slots, ("grp", "col"), axis=0, tiled=True)
    slot_values = gathered.reshape(grp_count, col_count, slot_width, PR, col_width)
    slot_values = slot_values.transpose(0, 2, 3, 1, 4).reshape(
        grp_count * slot_width, PR, col_count * col_width
    )
    flat_slots = slot_piece.reshape(-1)
    positions = jnp.arange(flat_slots.shape[0], dtype=jnp.int32)
    target = jnp.where(flat_slots >= 0, flat_slots, PIECES)
    piece_slot = jnp.zeros((PIECES + 1,), jnp.int32).at[target].set(positions)[:PIECES]
    weight_table = slot_values[piece_slot].reshape(PROWS, HID)
    encoder_weight = weight_table[:F]
    self_weight = weight_table[F : F + HID]
    neigh_weight = weight_table[F + HID : F + 2 * HID]
    head_weight = weight_table[F + 2 * HID : F + 2 * HID + CLS]
    encoder_bias = weight_table[PROWS - 2].astype(jnp.float32)
    sage_bias = weight_table[PROWS - 1].astype(jnp.float32)
    mask_values = loss_mask.astype(jnp.float32)
    labelled = lax.psum(jnp.sum(mask_values), ("grp", "col"))
    preact = jnp.dot(features, encoder_weight, preferred_element_type=jnp.float32) + encoder_bias
    sig_pre = jax.nn.sigmoid(preact)
    encoded = (preact * sig_pre).astype(jnp.bfloat16)
    enc_columns = lax.all_to_all(encoded, "col", split_axis=1, concat_axis=0, tiled=True)
    pairs = block_pairs[0]
    row_blocks = pairs[:, 0]
    col_blocks = pairs[:, 1]
    live_tiles = jnp.arange(tile_slots, dtype=jnp.int32) < tile_count[0]
    block_ids = jnp.arange(block_count, dtype=jnp.int32)
    row_places = ((row_blocks[None, :] == block_ids[:, None]) & live_tiles[None, :]).astype(
        jnp.float32
    )
    picked = enc_columns.reshape(block_count, B, -1)[col_blocks]
    products = jnp.einsum("tij,tjc->tic", adj_tiles, picked, preferred_element_type=jnp.float32)
    block_sums = jnp.einsum("rt,tic->ric", row_places, products, precision=lax.Precision.HIGHEST)
    degree_values = degree.astype(jnp.float32)
    mean_columns = (block_sums.reshape(group_nodes, -1) / degree_values[:, None]).astype(
        jnp.bfloat16
    )
    neigh_mean = lax.all_to_all(mean_columns, "col", split_axis=0, concat_axis=1, tiled=True)
    sage_pre = (
        jnp.dot(encoded, self_weight, preferred_element_type=jnp.float32)
        + jnp.dot(neigh_mean, neigh_weight, preferred_element_type=jnp.float32)
        + sage_bias
    )
    sig_sage = jax.nn.sigmoid(sage_pre)
    hidden = (sage_pre * sig_sage).astype(jnp.bfloat16)
    logits = contract_cols(hidden, head_weight)
    row_max = jnp.max(logits, axis=1, keepdims=True)
    log_total = row_max[:, 0] + jnp.log(jnp.sum(jnp.exp(logits - row_max), axis=1))
    label_hot = (labels[:, None] == jnp.arange(CLS, dtype=jnp.int32)[None, :]).astype(jnp.float32)
    target_logit = jnp.sum(logits * label_hot, axis=1)
    local_loss = jnp.sum(mask_values * (log_total - target_logit))
    probability = jnp.exp(logits - log_total[:, None])
    logit_grad = ((probability - label_hot) * mask_values[:, None] / labelled).astype(jnp.bfloat16)
    head_grad = contract_rows(logit_grad, hidden)
    hidden_grad = jnp.dot(logit_grad, head_weight, preferred_element_type=jnp.float32)
    sage_grad = (hidden_grad * sig_sage * (1.0 + sage_pre * (1.0 - sig_sage))).astype(jnp.bfloat16)
    self_grad = contract_rows(encoded, sage_grad)
    neigh_grad = contract_rows(neigh_mean, sage_grad)
    sage_bias_grad = jnp.sum(sage_grad.astype(jnp.float32), axis=0)
    self_back = contract_cols(sage_grad, self_weight)
    neigh_back = contract_cols(sage_grad, neigh_weight)
    degree_rows = lax.dynamic_slice_in_dim(degree_values, col_index * node_rows, node_rows)
    sum_grad = (neigh_back / degree_rows[:, None]).astype(jnp.bfloat16)
    grad_columns = lax.all_to_all(sum_grad, "col", split_axis=1, concat_axis=0, tiled=True)
    picked_grad = grad_columns.reshape(block_count, B, -1)[row_blocks]
    back_products = jnp.einsum(
        "tij,tic->tjc", adj_tiles, picked_grad, preferred_element_type=jnp.float32
    )
    col_places = ((col_blocks[None, :] == block_ids[:, None]) & live_tiles[None, :]).astype(
        jnp.float32
    )
    back_blocks = jnp.einsum(
        "rt,tjc->rjc", col_places, back_products, precision=lax.Precision.HIGHEST
    )
    neigh_return = lax.all_to_all(
        back_blocks.reshape(group_nodes, -1).astype(jnp.bfloat16),
        "col",
        split_axis=0,
        concat_axis=1,
        tiled=True,
    ).astype(jnp.float32)
    encoded_grad = self_back + neigh_return
    preact_grad = (encoded_grad * sig_pre * (1.0 + preact * (1.0 - sig_pre))).astype(jnp.bfloat16)
    encoder_grad = contract_rows(features, preact_grad)
    encoder_bias_grad = jnp.sum(preact_grad.astype(jnp.float32), axis=0)
    grad_table = jnp.concatenate(
        [
            encoder_grad,
            self_grad,
            neigh_grad,
            head_grad,
            encoder_bias_grad[None, :],
            sage_bias_grad[None, :],
        ],
        axis=0,
    )
    loss_total = lax.psum(local_loss, ("grp", "col"))
    mean_loss = loss_total / labelled
    group_grad = lax.psum_scatter(
        grad_table.astype(jnp.bfloat16), "col", scatter_dimension=1, tiled=True
    ).astype(jnp.float32)
    my_pieces = lax.dynamic_slice_in_dim(slot_piece, grp_index, 1, 0)[0]
    is_owned = my_pieces >= 0
    safe_pieces = jnp.where(is_owned, my_pieces, 0)
    owned_values = is_owned[:, None, None]
    total_grad = lax.psum(group_grad, "grp")
    slot_grad = jnp.where(owned_values, total_grad.reshape(PIECES, PR, -1)[safe_pieces], 0.0)
    table_rows = safe_pieces[:, None] * PR + jnp.arange(PR, dtype=jnp.int32)[None, :]
    decay_values = jnp.where(table_rows < PROWS - 2, decay_rate, 0.0)[:, :, None]
    first_moment = beta_one * moment_one + (1.0 - beta_one) * slot_grad
    second_moment = beta_two * moment_two + (1.0 - beta_two) * slot_grad * slot_grad
    first_hat = first_moment / (1.0 - beta_one**STEP)
    second_hat = second_moment / (1.0 - beta_two**STEP)
    updated = master - learn_rate * (
        first_hat / (jnp.sqrt(second_hat) + adam_epsilon) + decay_values * master
    )
    updated = jnp.where(owned_values, updated, 0.0)
    first_moment = jnp.where(owned_values, first_moment, 0.0)
    second_moment = jnp.where(owned_values, second_moment, 0.0)
    return (mean_loss, updated, first_moment, second_moment, updated.astype(jnp.bfloat16))


def solution(mesh):
    in_specs = (
        P(("grp", "col"), None),
        P("grp", None, None),
        P("grp", None, None),
        P("grp"),
        P("grp"),
        P(("grp", "col")),
        P(("grp", "col")),
        P(),
        P("grp", None, "col"),
        P("grp", None, "col"),
        P("grp", None, "col"),
    )
    out_specs = (
        P(),
        P("grp", None, "col"),
        P("grp", None, "col"),
        P("grp", None, "col"),
        P("grp", None, "col"),
    )
    return jax.shard_map(body, mesh=mesh, in_specs=in_specs, out_specs=out_specs, check_vma=False)
```

profile of v0, /device:TPU:0, one launch (start us, length us, event | category | flops | bytes accessed | tf_op | source)
XLA Modules:
  0.0 409.3 jit_solution(9063719519104682953)
XLA Ops:
  7.2 0.9 convert_element_type.70
  8.2 46.8 %all-gather = bf16[2528,2,64]{2,1,0:T(2,128)(2,1)S(1)} all-gather(bf16[79,2,64]{2,1,0:T(2,128)(2,1)S(1)} %copy.83), channel_id=2, replica_groups=mesh['grp'=8,'col'=4] {'grp','col'}, dimensions={0}, use_global_device_ids=true | all-gather | bytes 667392 | tf_op jit(solution)/shard_map/all_gather | solution.py:57
  55.0 1.1 copy.84
  56.1 0.8 reshape.171
  57.0 1.2 copy.85
  58.3 4.1 scatter_custom_fusion
  62.4 2.7 gather_fusion
  66.7 2.5 multiply_convert_fusion.1
  69.2 3.9 all-to-all-start
  73.9 13.6 %all-to-all-done = bf16[2048,4,64]{0,2,1:T(8,128)(2,1)S(1)} async-done(((bf16[2048,4,64]{0,2,1:T(8,128)(2,1)}), bf16[2048,4,64]{0,2,1:T(8,128)(2,1)S(1)}, u32[]{:S(2)}, u32[]{:S(2)}) %all-to-all-start) | async-done | bytes 1048608 | tf_op jit(solution)/shard_map/all_to_all | solution.py:78
  87.6 0.8 copy.86
  88.4 1.6 reshape.174
  89.9 1.8 copy.87
  91.8 8.0 %gather_fusion.1 = bf16[192,256,64]{1,2,0:T(8,128)(2,1)} fusion(bf16[32,256,64]{1,2,0:T(8,128)(2,1)S(1)} %copy.87, s32[1024]{0:T(1024)S(1)} %pad_clamp_fusion.2), kind=kCustom, calls=%fused_computation.1 | custom fusion | bytes 12583680 | tf_op jit(solution)/shard_map/gather | solution.py:87
  99.7 18.3 %convolution_bitcast_fusion.1 = f32[192,256,64]{1,2,0:T(8,128)} fusion(bf16[192,256,64]{1,2,0:T(8,128)(2,1)} %gather_fusion.1, bf16[192,256,256]{2,1,0:T(8,128)(2,1)} %param.12), kind=kOutput, calls=%fused_computation.10 | convolution fusion | flops 1610612736 | bytes 44040192 | tf_op jit(solution)/shard_map/tij,tjc->tic/dot_general | solution.py:88
  118.1 16.9 %fusion.2 = f32[32,256,64]{1,0,2:T(8,128)} fusion(f32[192,256,64]{1,2,0:T(8,128)} %convolution_bitcast_fusion.1, s32[192]{0:T(256)S(1)} %bitcast.95, pred[192]{0:T(512)(128)(4,1)S(1)} %iota_compare_fusion.3), kind=kOutput, calls=%fused_computation.7 | convolution fusion | flops 1207971840 | bytes 14681024 | tf_op jit(solution)/shard_map/rt,tic->ric/dot_general | solution.py:89
  134.9 2.2 reshape.175
  137.1 2.1 fusion.12
  139.3 3.6 all-to-all-start.1
  143.1 3.0 fusion.40
  146.2 11.1 %all-to-all-done.1 = bf16[4,2048,64]{1,2,0:T(8,128)(2,1)S(1)} async-done(((bf16[4,2048,64]{1,2,0:T(8,128)(2,1)}), bf16[4,2048,64]{1,2,0:T(8,128)(2,1)S(1)}, u32[]{:S(2)}, u32[]{:S(2)}) %all-to-all-start.1) | async-done | bytes 1048608 | tf_op jit(solution)/shard_map/all_to_all | solution.py:94
  157.3 3.7 multiply_convert_fusion
  161.0 1.0 copy-done.6
  163.1 37.2 %all-reduce = (f32[]{:T(128)}, f32[]{:T(128)}) all-reduce(f32[]{:T(128)} %get-tuple-element.27, f32[]{:T(128)} %get-tuple-element.28), channel_id=1, replica_groups=mesh['grp'=8,'col'=4] {'grp','col'}, use_global_device_ids=true, to_apply=%region_7.8 | all-reduce | flops 2 | bytes 16 | tf_op jit(solution)/shard_map/psum | solution.py:74
  200.4 3.4 fusion.39
  203.8 1.4 fusion.10
  205.2 3.5 all-to-all-start.2
  208.8 14.4 %all-to-all-done.2 = bf16[2048,4,64]{0,2,1:T(8,128)(2,1)S(1)} async-done(((bf16[2048,4,64]{0,2,1:T(8,128)(2,1)}), bf16[2048,4,64]{0,2,1:T(8,128)(2,1)S(1)}, u32[]{:S(2)}, u32[]{:S(2)}) %all-to-all-start.2) | async-done | bytes 1048608 | tf_op jit(solution)/shard_map/all_to_all | solution.py:120
  223.2 1.8 copy.94
  225.0 2.6 reshape.176
  227.6 1.8 copy.95
  229.4 8.0 %gather_fusion.2 = bf16[192,256,64]{1,2,0:T(8,128)(2,1)} fusion(bf16[32,256,64]{1,2,0:T(8,128)(2,1)S(1)} %copy.95, s32[1024]{0:T(1024)S(1)} %pad_clamp_fusion.1), kind=kCustom, calls=%fused_computation.2 | custom fusion | bytes 12583680 | tf_op jit(solution)/shard_map/gather | solution.py:121
  237.3 19.0 %convolution_bitcast_fusion = f32[192,256,64]{1,2,0:T(8,128)} fusion(bf16[192,256,64]{1,2,0:T(8,128)(2,1)} %gather_fusion.2, bf16[192,256,256]{2,1,0:T(8,128)(2,1)} %param.12), kind=kOutput, calls=%fused_computation.9 | convolution fusion | flops 1610612736 | bytes 44040192 | tf_op jit(solution)/shard_map/tij,tic->tjc/dot_general | solution.py:122
  256.3 16.4 %fusion.13 = bf16[32,256,64]{1,0,2:T(8,128)(2,1)} fusion(f32[192,256,64]{1,2,0:T(8,128)} %convolution_bitcast_fusion, s32[192]{0:T(256)S(1)} %bitcast.94, pred[192]{0:T(512)(128)(4,1)S(1)} %iota_compare_fusion.3), kind=kOutput, calls=%fused_computation.30 | convolution fusion | flops 1208496128 | bytes 13632448 | tf_op jit(solution)/shard_map/rt,tjc->rjc/dot_general | solution.py:128
  272.8 1.9 convert_element_type.80
  274.6 1.6 copy.97
  276.2 3.5 all-to-all-start.3
  279.8 3.2 convolution_convert_fusion.3
  283.4 1.7 convolution_convert_fusion.1
  285.1 9.0 %all-to-all-done.3 = bf16[4,2048,64]{1,2,0:T(8,128)(2,1)S(1)} async-done(((bf16[4,2048,64]{1,2,0:T(8,128)(2,1)}), bf16[4,2048,64]{1,2,0:T(8,128)(2,1)S(1)}, u32[]{:S(2)}, u32[]{:S(2)}) %all-to-all-start.3) | async-done | bytes 1048608 | tf_op jit(solution)/shard_map/all_to_all | solution.py:131
  294.4 1.3 copy-done.18
  295.7 1.2 fusion.38
  297.7 1.0 copy.110
  299.1 21.4 %reduce-scatter.4.cloned.1.call-done = bf16[64,834]{1,0:T(8,128)(2,1)} async-done(((bf16[256,834]{1,0:T(8,128)(2,1)}), bf16[64,834]{1,0:T(8,128)(2,1)}) %reduce-scatter.4.cloned.1.call-update) | async-done | bytes 106768
  320.6 1.1 copy.111
  321.7 1.0 reshape.177
  324.1 71.9 %all-reduce.3.cloned.1.call-done = f32[417,2,64]{2,1,0:T(2,128)} async-done(((f32[417,2,64]{2,1,0:T(2,128)}), f32[417,2,64]{2,1,0:T(2,128)}) %all-reduce.3.cloned.1.call-update) | async-done | bytes 213520 | tf_op jit(solution)/shard_map/psum | solution.py:162
  396.1 1.7 gather_fusion.3
  (86 shorter events, 8.5 us)
Async XLA Ops:
  7.2 59.5 %copy-start = (bf16[2048,256]{1,0:T(8,128)(2,1)S(1)}, bf16[2048,256]{1,0:T(8,128)(2,1)}, u32[]{:S(2)}) copy-start(bf16[2048,256]{1,0:T(8,128)(2,1)} %param.11) | copy-start | bytes 3145732
  55.0 3.2 copy-start.15
  65.1 4.1 %copy-start.4 = (bf16[417,2,256]{2,1,0:T(2,128)(2,1)}, bf16[417,2,256]{2,1,0:T(2,128)(2,1)S(1)}, u32[]{:S(2)}) copy-start(bf16[417,2,256]{2,1,0:T(2,128)(2,1)S(1)} %gather_fusion) | copy-start | bytes 1281028
  69.2 4.6 %copy-start.11 = (s32[8192]{0:T(1024)S(1)}, s32[8192]{0:T(1024)}, u32[]{:S(2)}) copy-start(s32[8192]{0:T(1024)} %param.15) | copy-start | bytes 98308
  69.2 4.7 %copy-start.16 = (s32[1,192,2]{1,2,0:T(2,128)S(1)}, s32[1,192,2]{1,2,0:T(2,128)}, u32[]{:S(2)}) copy-start(s32[1,192,2]{1,2,0:T(2,128)} %param.13) | copy-start | bytes 4612
  69.2 18.3 %all-to-all-start = ((bf16[2048,4,64]{0,2,1:T(8,128)(2,1)}), bf16[2048,4,64]{0,2,1:T(8,128)(2,1)S(1)}, u32[]{:S(2)}, u32[]{:S(2)}) async-start(bf16[2048,4,64]{0,2,1:T(8,128)(2,1)} %bitcast.8), calls=%async_computation | async-start | bytes 2097152 | tf_op jit(solution)/shard_map/all_to_all | solution.py:78
  73.9 13.7 %copy-start.8 = (f32[8192]{0:T(1024)}, f32[8192]{0:T(1024)S(1)}, u32[]{:S(2)}) copy-start(f32[8192]{0:T(1024)S(1)} %convert_element_type.72) | copy-start | bytes 98308
  139.2 3.8 slice-start
  139.2 3.8 copy-start.12
  139.3 18.1 %all-to-all-start.1 = ((bf16[4,2048,64]{1,2,0:T(8,128)(2,1)}), bf16[4,2048,64]{1,2,0:T(8,128)(2,1)S(1)}, u32[]{:S(2)}, u32[]{:S(2)}) async-start(bf16[4,2048,64]{1,2,0:T(8,128)(2,1)} %fusion.12), calls=%async_computation.1 | async-start | bytes 2097152 | tf_op jit(solution)/shard_map/all_to_all | solution.py:94
  142.9 14.4 %copy-start.17 = (f32[1,256]{1,0:T(1,128)S(1)}, f32[1,256]{1,0:T(1,128)}, u32[]{:S(2)}) copy-start(f32[1,256]{1,0:T(1,128)} %get-tuple-element.34) | copy-start | bytes 3076
  157.3 5.0 %copy-start.14 = (s32[2048]{0:T(1024)S(1)}, s32[2048]{0:T(1024)}, u32[]{:S(2)}) copy-start(s32[2048]{0:T(1024)} %param.16) | copy-start | bytes 24580
  161.0 1.0 copy-start.6
  162.3 41.4 %copy-start.5 = (f32[2048,64]{0,1:T(8,128)}, f32[2048,64]{0,1:T(8,128)S(1)}, u32[]{:S(2)}) copy-start(f32[2048,64]{0,1:T(8,128)S(1)} %get-tuple-element.50) | copy-start | bytes 1572868
  200.4 3.4 dynamic-slice-start
  203.8 1.5 copy-start.1
  205.2 18.0 %all-to-all-start.2 = ((bf16[2048,4,64]{0,2,1:T(8,128)(2,1)}), bf16[2048,4,64]{0,2,1:T(8,128)(2,1)S(1)}, u32[]{:S(2)}, u32[]{:S(2)}) async-start(bf16[2048,4,64]{0,2,1:T(8,128)(2,1)} %bitcast.92), calls=%async_computation.2 | async-start | bytes 2097152 | tf_op jit(solution)/shard_map/all_to_all | solution.py:120
  276.2 17.9 %all-to-all-start.3 = ((bf16[4,2048,64]{1,2,0:T(8,128)(2,1)}), bf16[4,2048,64]{1,2,0:T(8,128)(2,1)S(1)}, u32[]{:S(2)}, u32[]{:S(2)}) async-start(bf16[4,2048,64]{1,2,0:T(8,128)(2,1)} %copy.97), calls=%async_computation.3 | async-start | bytes 2097152 | tf_op jit(solution)/shard_map/all_to_all | solution.py:131
  279.7 40.9 %reduce-scatter.4.cloned.1.call-start = ((), (), s32[]{:S(2)}) async-start(), calls=%async_computation.6 | async-start | bytes 573440
  279.7 3.2 copy-start.2
  285.1 9.2 %copy-start.3 = (bf16[2048,256]{0,1:T(8,128)(2,1)S(1)}, bf16[2048,256]{0,1:T(8,128)(2,1)}, u32[]{:S(2)}) copy-start(bf16[2048,256]{0,1:T(8,128)(2,1)} %copy-done.1) | copy-start | bytes 3145732
  294.1 1.6 copy-start.18
  296.9 0.8 copy-start.13
  296.9 1.9 copy-start.7
  296.9 2.0 copy-start.9
  296.9 2.1 copy-start.10
  298.7 97.4 %all-reduce.3.cloned.1.call-start = ((), (), s32[]{:S(2)}) async-start(), calls=%async_computation.5 | async-start | bytes 854016 | tf_op jit(solution)/shard_map/psum | solution.py:162
Sparse Core Ops, SparseCore 0:
  298.8 21.7 reduce-scatter.3
  324.0 72.0 all-reduce.2
where the time goes:
time: 415 us; the launch traced here: 409 us
  waiting for transfers between devices  142 us (34%)
  matrix products  92.1 us (22%)
  blocking collectives  84 us (20%)
  local copies, waits for them, and re-layouts  53.8 us (13%)
  between operations  17.9 us (4%)
  starting transfers between devices  14.7 us (4%)
  other arithmetic  5.23 us (1%)
    psum x1, waiting for transfers between devices, body(): total_grad = lax.psum(group_grad, 'grp')  71.9 us
    all_gather x1, blocking collectives, body(): gathered = lax.all_gather(own_slots, ('grp', 'col'), axis=0, tiled=True)  46.8 us
    psum x1, blocking collectives, body(): labelled = lax.psum(jnp.sum(mask_values), ('grp', 'col'))  37.2 us
    unnamed x3, waiting for transfers between devices  21.5 us
    dot_general x1, matrix products, body(): jnp.einsum('tij,tic->tjc', adj_tiles, picked_grad, preferred_element_type...  19 us
    dot_general x1, matrix products, body(): jnp.einsum('tij,tjc->tic', adj_tiles, picked, preferred_element_type=jnp....  18.3 us
    dot_general x1, matrix products, body(): jnp.einsum('rt,tic->ric', row_places, products, precision=lax.Precision.H...  16.9 us
    dot_general x1, matrix products, body(): jnp.einsum('rt,tjc->rjc', col_places, back_products, precision=lax.Precis...  16.4 us
  transfers between devices with their start and end apart: 6, of which 6 were waited for; matrix products, arithmetic and copies ran while one was open for 2% of the time, Pallas kernels for 0%

commit v1 on v0

--- a/solution.py
+++ b/solution.py
@@ -159,7 +159,7 @@
     is_owned = my_pieces >= 0
     safe_pieces = jnp.where(is_owned, my_pieces, 0)
     owned_values = is_owned[:, None, None]
-    total_grad = lax.psum(group_grad, "grp")
+    total_grad = lax.all_gather(group_grad, axis_name="grp").sum(axis=0)
     slot_grad = jnp.where(owned_values, total_grad.reshape(PIECES, PR, -1)[safe_pieces], 0.0)
     table_rows = safe_pieces[:, None] * PR + jnp.arange(PR, dtype=jnp.int32)[None, :]
     decay_values = jnp.where(table_rows < PROWS - 2, decay_rate, 0.0)[:, :, None]

time: 415 us -> 389 us (0.937)
  waiting for transfers between devices: 142 us -> 115 us
    psum x1 -> x0, waiting for transfers between devices: 71.9 us -> none  [body(): total_grad = lax.psum(group_grad, 'grp')]
    all_gather x0 -> x1, waiting for transfers between devices: none -> 44.7 us  [body(): total_grad = lax.all_gather(group_grad, axis_name='grp').sum(axis=0)]
    unnamed x47 -> x48, local copies, waits for them, and re-layouts: 7.83 us -> 8.77 us
where the time goes in v1:
time: 389 us; the launch traced here: 383 us
  waiting for transfers between devices  115 us (30%)
  matrix products  92.1 us (24%)
  blocking collectives  84 us (22%)
  local copies, waits for them, and re-layouts  53.1 us (14%)
  between operations  17.9 us (5%)
  starting transfers between devices  14.7 us (4%)
  other arithmetic  6.88 us (2%)
    all_gather x1, blocking collectives, body(): gathered = lax.all_gather(own_slots, ('grp', 'col'), axis=0, tiled=True)  46.8 us
    all_gather x1, waiting for transfers between devices, body(): total_grad = lax.all_gather(group_grad, axis_name='grp').sum(axis=0)  44.7 us
    psum x1, blocking collectives, body(): loss_total = lax.psum(local_loss, ('grp', 'col'))  37.2 us
    unnamed x3, waiting for transfers between devices  21.9 us
    dot_general x1, matrix products, body(): jnp.einsum('tij,tic->tjc', adj_tiles, picked_grad, preferred_element_type...  19 us
    dot_general x1, matrix products, body(): jnp.einsum('tij,tjc->tic', adj_tiles, picked, preferred_element_type=jnp....  18.3 us
    dot_general x1, matrix products, body(): jnp.einsum('rt,tic->ric', row_places, products, precision=lax.Precision.H...  16.9 us
    dot_general x1, matrix products, body(): jnp.einsum('rt,tjc->rjc', col_places, back_products, precision=lax.Precis...  16.4 us
  transfers between devices with their start and end apart: 6, of which 6 were waited for; matrix products, arithmetic and copies ran while one was open for 2% of the time, Pallas kernels for 0%

profile of v1, /device:TPU:0, one launch (start us, length us, event | category | flops | bytes accessed | tf_op | source)
XLA Modules:
  0.0 383.5 jit_solution(1021148369344006423)
XLA Ops:
  7.2 0.9 convert_element_type.68
  8.2 46.8 %all-gather = bf16[2528,2,64]{2,1,0:T(2,128)(2,1)S(1)} all-gather(bf16[79,2,64]{2,1,0:T(2,128)(2,1)S(1)} %copy.109), channel_id=2, replica_groups=mesh['grp'=8,'col'=4] {'grp','col'}, dimensions={0}, use_global_device_ids=true | all-gather | bytes 667392 | tf_op jit(solution)/shard_map/all_gather | solution.py:57
  55.0 1.1 copy.110
  56.1 0.8 reshape.171
  57.0 1.2 copy.111
  58.3 4.1 %scatter_custom_fusion = s32[418]{0:T(512)S(1)} fusion(s32[632]{0:T(1024)S(1)} %fusion.29, s32[632]{0:T(1024)S(1)} %iota.23, s32[]{:T(128)} %constant.21.clone.1), kind=kCustom, calls=%fused_computation.77 | custom fusion | bytes 1676 | tf_op jit(solution)/shard_map/scatter | solution.py:65
  62.4 2.7 gather_fusion
  66.7 2.5 multiply_convert_fusion.1
  69.2 3.9 %all-to-all-start = ((bf16[2048,4,64]{0,2,1:T(8,128)(2,1)}), bf16[2048,4,64]{0,2,1:T(8,128)(2,1)S(1)}, u32[]{:S(2)}, u32[]{:S(2)}) async-start(bf16[2048,4,64]{0,2,1:T(8,128)(2,1)} %bitcast.8), calls=%async_computation | async-start | bytes 2097152 | tf_op jit(solution)/shard_map/all_to_all | solution.py:78
  73.9 13.6 %all-to-all-done = bf16[2048,4,64]{0,2,1:T(8,128)(2,1)S(1)} async-done(((bf16[2048,4,64]{0,2,1:T(8,128)(2,1)}), bf16[2048,4,64]{0,2,1:T(8,128)(2,1)S(1)}, u32[]{:S(2)}, u32[]{:S(2)}) %all-to-all-start) | async-done | bytes 1048608 | tf_op jit(solution)/shard_map/all_to_all | solution.py:78
  87.6 0.8 copy.112
  88.4 1.6 reshape.174
  89.9 1.8 copy.113
  91.8 8.0 %gather_fusion.1 = bf16[192,256,64]{1,2,0:T(8,128)(2,1)} fusion(bf16[32,256,64]{1,2,0:T(8,128)(2,1)S(1)} %copy.113, s32[1024]{0:T(1024)S(1)} %pad_clamp_fusion.2), kind=kCustom, calls=%fused_computation.1 | custom fusion | bytes 12583680 | tf_op jit(solution)/shard_map/gather | solution.py:87
  99.7 18.3 %convolution_bitcast_fusion.1 = f32[192,256,64]{1,2,0:T(8,128)} fusion(bf16[192,256,64]{1,2,0:T(8,128)(2,1)} %gather_fusion.1, bf16[192,256,256]{2,1,0:T(8,128)(2,1)} %param.12), kind=kOutput, calls=%fused_computation.10 | convolution fusion | flops 1610612736 | bytes 44040192 | tf_op jit(solution)/shard_map/tij,tjc->tic/dot_general | solution.py:88
  118.1 16.9 %fusion.2 = f32[32,256,64]{1,0,2:T(8,128)} fusion(f32[192,256,64]{1,2,0:T(8,128)} %convolution_bitcast_fusion.1, s32[192]{0:T(256)S(1)} %bitcast.98, pred[192]{0:T(512)(128)(4,1)S(1)} %iota_compare_fusion.3), kind=kOutput, calls=%fused_computation.7 | convolution fusion | flops 1207971840 | bytes 14681024 | tf_op jit(solution)/shard_map/rt,tic->ric/dot_general | solution.py:89
  134.9 2.2 reshape.175
  137.1 2.1 fusion.12
  139.3 3.6 all-to-all-start.1
  143.1 3.0 fusion.40
  146.2 11.1 %all-to-all-done.1 = bf16[4,2048,64]{1,2,0:T(8,128)(2,1)S(1)} async-done(((bf16[4,2048,64]{1,2,0:T(8,128)(2,1)}), bf16[4,2048,64]{1,2,0:T(8,128)(2,1)S(1)}, u32[]{:S(2)}, u32[]{:S(2)}) %all-to-all-start.1) | async-done | bytes 1048608 | tf_op jit(solution)/shard_map/all_to_all | solution.py:94
  157.3 3.7 multiply_convert_fusion
  161.0 1.0 copy-done.6
  163.1 37.2 %all-reduce = (f32[]{:T(128)}, f32[]{:T(128)}) all-reduce(f32[]{:T(128)} %get-tuple-element.33, f32[]{:T(128)} %get-tuple-element.32), channel_id=1, replica_groups=mesh['grp'=8,'col'=4] {'grp','col'}, use_global_device_ids=true, to_apply=%region_5.6 | all-reduce | flops 2 | bytes 16 | tf_op jit(solution)/shard_map/psum | solution.py:153
  200.4 3.4 fusion.39
  203.8 1.4 fusion.10
  205.2 3.5 all-to-all-start.2
  208.8 14.4 %all-to-all-done.2 = bf16[2048,4,64]{0,2,1:T(8,128)(2,1)S(1)} async-done(((bf16[2048,4,64]{0,2,1:T(8,128)(2,1)}), bf16[2048,4,64]{0,2,1:T(8,128)(2,1)S(1)}, u32[]{:S(2)}, u32[]{:S(2)}) %all-to-all-start.2) | async-done | bytes 1048608 | tf_op jit(solution)/shard_map/all_to_all | solution.py:120
  223.2 1.8 copy.120
  225.0 2.6 reshape.176
  227.6 1.8 copy.121
  229.4 8.0 %gather_fusion.2 = bf16[192,256,64]{1,2,0:T(8,128)(2,1)} fusion(bf16[32,256,64]{1,2,0:T(8,128)(2,1)S(1)} %copy.121, s32[1024]{0:T(1024)S(1)} %pad_clamp_fusion.1), kind=kCustom, calls=%fused_computation.2 | custom fusion | bytes 12583680 | tf_op jit(solution)/shard_map/gather | solution.py:121
  237.3 19.0 %convolution_bitcast_fusion = f32[192,256,64]{1,2,0:T(8,128)} fusion(bf16[192,256,64]{1,2,0:T(8,128)(2,1)} %gather_fusion.2, bf16[192,256,256]{2,1,0:T(8,128)(2,1)} %param.12), kind=kOutput, calls=%fused_computation.9 | convolution fusion | flops 1610612736 | bytes 44040192 | tf_op jit(solution)/shard_map/tij,tic->tjc/dot_general | solution.py:122
  256.3 16.4 %fusion.13 = bf16[32,256,64]{1,0,2:T(8,128)(2,1)} fusion(f32[192,256,64]{1,2,0:T(8,128)} %convolution_bitcast_fusion, s32[192]{0:T(256)S(1)} %bitcast.97, pred[192]{0:T(512)(128)(4,1)S(1)} %iota_compare_fusion.3), kind=kOutput, calls=%fused_computation.30 | convolution fusion | flops 1208496128 | bytes 13632448 | tf_op jit(solution)/shard_map/rt,tjc->rjc/dot_general | solution.py:128
  272.8 1.9 convert_element_type.78
  274.6 1.6 copy.123
  276.2 3.5 all-to-all-start.3
  279.8 3.2 convolution_convert_fusion.3
  283.4 1.7 convolution_convert_fusion.1
  285.1 9.0 %all-to-all-done.3 = bf16[4,2048,64]{1,2,0:T(8,128)(2,1)S(1)} async-done(((bf16[4,2048,64]{1,2,0:T(8,128)(2,1)}), bf16[4,2048,64]{1,2,0:T(8,128)(2,1)S(1)}, u32[]{:S(2)}, u32[]{:S(2)}) %all-to-all-start.3) | async-done | bytes 1048608 | tf_op jit(solution)/shard_map/all_to_all | solution.py:131
  294.4 1.3 copy-done.18
  295.7 1.2 fusion.38
  297.7 1.0 copy.138
  298.7 21.9 %reduce-scatter.4.cloned.1.call-done = bf16[64,834]{1,0:T(8,128)(2,1)} async-done(((bf16[256,834]{1,0:T(8,128)(2,1)}), bf16[64,834]{1,0:T(8,128)(2,1)}) %reduce-scatter.4.cloned.1.call-update) | async-done | bytes 106768
  320.6 1.1 copy.139
  321.7 0.9 copy.125
  324.5 44.7 %all-gather.5.cloned.1.call-done = f32[8,834,64]{1,2,0:T(8,128)} async-done(((f32[1,834,64]{1,2,0:T(8,128)}), f32[8,834,64]{1,2,0:T(8,128)}) %all-gather.5.cloned.1.call-update) | async-done | bytes 1708048 | tf_op jit(solution)/shard_map/all_gather | solution.py:162
  369.2 1.6 reduce_sum.69
  (90 shorter events, 9.6 us)
Async XLA Ops:
  7.2 59.5 %copy-start = (bf16[2048,256]{1,0:T(8,128)(2,1)S(1)}, bf16[2048,256]{1,0:T(8,128)(2,1)}, u32[]{:S(2)}) copy-start(bf16[2048,256]{1,0:T(8,128)(2,1)} %param.11) | copy-start | bytes 3145732
  55.0 3.2 copy-start.15
  65.1 4.1 %copy-start.4 = (bf16[417,2,256]{2,1,0:T(2,128)(2,1)}, bf16[417,2,256]{2,1,0:T(2,128)(2,1)S(1)}, u32[]{:S(2)}) copy-start(bf16[417,2,256]{2,1,0:T(2,128)(2,1)S(1)} %gather_fusion) | copy-start | bytes 1281028
  69.2 4.6 %copy-start.11 = (s32[8192]{0:T(1024)S(1)}, s32[8192]{0:T(1024)}, u32[]{:S(2)}) copy-start(s32[8192]{0:T(1024)} %param.15) | copy-start | bytes 98308
  69.2 4.7 %copy-start.16 = (s32[1,192,2]{1,2,0:T(2,128)S(1)}, s32[1,192,2]{1,2,0:T(2,128)}, u32[]{:S(2)}) copy-start(s32[1,192,2]{1,2,0:T(2,128)} %param.13) | copy-start | bytes 4612
  69.2 18.3 %all-to-all-start = ((bf16[2048,4,64]{0,2,1:T(8,128)(2,1)}), bf16[2048,4,64]{0,2,1:T(8,128)(2,1)S(1)}, u32[]{:S(2)}, u32[]{:S(2)}) async-start(bf16[2048,4,64]{0,2,1:T(8,128)(2,1)} %bitcast.8), calls=%async_computation | async-start | bytes 2097152 | tf_op jit(solution)/shard_map/all_to_all | solution.py:78
  73.9 13.7 %copy-start.8 = (f32[8192]{0:T(1024)}, f32[8192]{0:T(1024)S(1)}, u32[]{:S(2)}) copy-start(f32[8192]{0:T(1024)S(1)} %convert_element_type.70) | copy-start | bytes 98308
  139.2 3.8 slice-start
  139.2 3.8 copy-start.12
  139.3 18.1 %all-to-all-start.1 = ((bf16[4,2048,64]{1,2,0:T(8,128)(2,1)}), bf16[4,2048,64]{1,2,0:T(8,128)(2,1)S(1)}, u32[]{:S(2)}, u32[]{:S(2)}) async-start(bf16[4,2048,64]{1,2,0:T(8,128)(2,1)} %fusion.12), calls=%async_computation.1 | async-start | bytes 2097152 | tf_op jit(solution)/shard_map/all_to_all | solution.py:94
  142.9 14.4 %copy-start.17 = (f32[1,256]{1,0:T(1,128)S(1)}, f32[1,256]{1,0:T(1,128)}, u32[]{:S(2)}) copy-start(f32[1,256]{1,0:T(1,128)} %get-tuple-element.39) | copy-start | bytes 3076
  157.3 5.0 %copy-start.14 = (s32[2048]{0:T(1024)S(1)}, s32[2048]{0:T(1024)}, u32[]{:S(2)}) copy-start(s32[2048]{0:T(1024)} %param.16) | copy-start | bytes 24580
  161.0 1.0 copy-start.6
  162.3 41.4 %copy-start.5 = (f32[2048,64]{0,1:T(8,128)}, f32[2048,64]{0,1:T(8,128)S(1)}, u32[]{:S(2)}) copy-start(f32[2048,64]{0,1:T(8,128)S(1)} %get-tuple-element.55) | copy-start | bytes 1572868
  200.4 3.4 dynamic-slice-start
  203.8 1.5 copy-start.1
  205.2 18.0 %all-to-all-start.2 = ((bf16[2048,4,64]{0,2,1:T(8,128)(2,1)}), bf16[2048,4,64]{0,2,1:T(8,128)(2,1)S(1)}, u32[]{:S(2)}, u32[]{:S(2)}) async-start(bf16[2048,4,64]{0,2,1:T(8,128)(2,1)} %bitcast.95), calls=%async_computation.2 | async-start | bytes 2097152 | tf_op jit(solution)/shard_map/all_to_all | solution.py:120
  276.2 17.9 %all-to-all-start.3 = ((bf16[4,2048,64]{1,2,0:T(8,128)(2,1)}), bf16[4,2048,64]{1,2,0:T(8,128)(2,1)S(1)}, u32[]{:S(2)}, u32[]{:S(2)}) async-start(bf16[4,2048,64]{1,2,0:T(8,128)(2,1)} %copy.123), calls=%async_computation.3 | async-start | bytes 2097152 | tf_op jit(solution)/shard_map/all_to_all | solution.py:131
  279.7 40.9 %reduce-scatter.4.cloned.1.call-start = ((), (), s32[]{:S(2)}) async-start(), calls=%async_computation.6 | async-start | bytes 573440
  279.7 3.2 copy-start.2
  285.1 9.2 %copy-start.3 = (bf16[2048,256]{0,1:T(8,128)(2,1)S(1)}, bf16[2048,256]{0,1:T(8,128)(2,1)}, u32[]{:S(2)}) copy-start(bf16[2048,256]{0,1:T(8,128)(2,1)} %copy-done.1) | copy-start | bytes 3145732
  294.1 1.6 copy-start.18
  296.9 0.8 copy-start.13
  297.4 25.2 %copy-start.7 = (f32[79,2,64]{0,2,1:T(8,128)S(1)}, f32[79,2,64]{0,2,1:T(8,128)}, u32[]{:S(2)}) copy-start(f32[79,2,64]{0,2,1:T(8,128)} %param.19) | copy-start | bytes 121348
  297.6 25.1 %copy-start.9 = (f32[79,2,64]{0,2,1:T(8,128)S(1)}, f32[79,2,64]{0,2,1:T(8,128)}, u32[]{:S(2)}) copy-start(f32[79,2,64]{0,2,1:T(8,128)} %param.20) | copy-start | bytes 121348
  297.6 25.3 %copy-start.10 = (f32[79,2,64]{0,2,1:T(8,128)S(1)}, f32[79,2,64]{0,2,1:T(8,128)}, u32[]{:S(2)}) copy-start(f32[79,2,64]{0,2,1:T(8,128)} %param.21) | copy-start | bytes 121348
  298.7 70.5 %all-gather.5.cloned.1.call-start = ((), (), s32[]{:S(2)}) async-start(), calls=%async_computation.5 | async-start | bytes 2064384 | tf_op jit(solution)/shard_map/all_gather | solution.py:162
Sparse Core Ops, SparseCore 0:
  298.8 21.7 reduce-scatter.3
  322.8 46.3 all-gather.4
